TPU v7x, 32 devices: a whole 2x2x4 slice. The times are simulated.
32 devices in a mesh: fsdp: 8 (over z, x), tp: 4 (over y, core).
Axes of the slice: x: 2, y: 2, z: 4, core: 2. Of those that a mesh axis runs over, the one named last changes fastest.
Arguments:
- slopes_in: float32 [32, 128, 4096], P(None, 'fsdp', 'tp'), may hold values from -6 to 6
- moments_in: float32 [32, 128, 4096], P(None, 'fsdp', 'tp'), may hold values from -6 to 6
- weights_in: float32 [32, 128, 4096], P(None, 'fsdp', 'tp'), may hold values from -0.1875 to 0.1875
Outputs:
- new_weights: float32 [32, 128, 4096], P(None, 'fsdp', 'tp')
- new_momentum: float32 [32, 128, 4096], P(None, 'fsdp', 'tp')
All inputs are finite; a program needn't handle non-finite values.
Results may differ from a plain program's by a relative error of at most 0.00021.
Values sent between devices are 32-bit elements; how exact they have to be, the bound alone decides.
A program may use at most 128 MiB of HBM per device.

v0:
```python
import jax
import jax.numpy as jnp
from jax import lax
from jax.sharding import PartitionSpec as P

ITERS = 5
hold_rate = 0.8
learn_rate = 1.0


def body(slopes_in, moments_in, weights_in):
    new_momentum = hold_rate * moments_in + slopes_in
    moved = lax.all_to_all(new_momentum, "fsdp", split_axis=0, concat_axis=1, tiled=True)
    whole = lax.all_to_all(moved, "tp", split_axis=0, concat_axis=2, tiled=True)
    iterate = whole * lax.rsqrt(jnp.sum(whole * whole, axis=(1, 2), keepdims=True) + 1e-06)
    for step in range(ITERS):
        gram = jnp.einsum("mik,mjk->mij", iterate, iterate, precision=lax.Precision.HIGHEST)
        mixed = -4.775 * gram + 2.0315 * jnp.einsum(
            "mij,mjk->mik", gram, gram, precision=lax.Precision.HIGHEST
        )
        iterate = 3.4445 * iterate + jnp.einsum(
            "mij,mjk->mik", mixed, iterate, precision=lax.Precision.HIGHEST
        )
    iterate = lax.all_to_all(iterate, "tp", split_axis=2, concat_axis=0, tiled=True)
    back = lax.all_to_all(iterate, "fsdp", split_axis=1, concat_axis=0, tiled=True)
    new_weights = weights_in - learn_rate * back
    return (new_weights, new_momentum)


def solution(mesh):
    return jax.shard_map(
        body,
        mesh=mesh,
        in_specs=(P(None, "fsdp", "tp"), P(None, "fsdp", "tp"), P(None, "fsdp", "tp")),
        out_specs=(P(None, "fsdp", "tp"), P(None, "fsdp", "tp")),
        check_vma=False,
    )
```

profile of v0, /device:TPU:0, one launch (start us, length us, event | category | flops | bytes accessed | tf_op | source)
XLA Modules:
  0.0 212.4 jit_solution(16108924228545123372)
XLA Ops:
  0.6 2.7 %multiply_add_fusion = f32[32,16,1024]{2,1,0:T(8,128)S(1)} fusion(f32[32,16,1024]{2,1,0:T(8,128)} %param.3, f32[32,16,1024]{2,1,0:T(8,128)} %param.4), kind=kLoop, calls=%fused_computation.11 | loop fusion | flops 1048576 | bytes 6291456 | tf_op jit(solution)/shard_map/add | solution.py:12
  3.3 55.3 %all_to_all.63 = f32[32,16,1024]{2,1,0:T(8,128)S(1)} all-to-all(f32[32,16,1024]{2,1,0:T(8,128)S(1)} %multiply_add_fusion), channel_id=1, replica_groups=mesh['fsdp'=8,'tp'=4] {'fsdp'}, dimensions={0} | all-to-all | bytes 4194304 | tf_op jit(solution)/shard_map/all_to_all | solution.py:13
  58.9 28.3 %all_to_all.64 = f32[4,128,1024]{2,1,0:T(8,128)S(1)} all-to-all(f32[4,128,1024]{2,1,0:T(8,128)S(1)} %bitcast.63), channel_id=1, replica_groups=mesh['fsdp'=8,'tp'=4] {'tp'}, dimensions={0} | all-to-all | bytes 4194304 | tf_op jit(solution)/shard_map/all_to_all | solution.py:14
  88.9 1.8 fusion.4
  91.0 2.6 %multiply_bitcast_fusion.1 = (f32[1,128,4,1024]{3,1,2,0:T(8,128)}, f32[1,128,4,1024]{3,1,2,0:T(8,128)}) fusion(f32[4,128,1024]{2,1,0:T(8,128)S(1)} %all_to_all.64, f32[]{:T(128)S(6)} %rsqrt.4), kind=kLoop, calls=%fused_computation.13 | loop fusion | flops 1048576 | bytes 6291460 | tf_op jit(solution)/shard_map/mul | solution.py:15
  93.5 1.9 copy.32
  95.4 2.9 %copy.31 = f32[1,128,4,1024]{1,3,2,0:T(8,128)} copy(f32[1,128,4,1024]{3,1,2,0:T(8,128)} %get-tuple-element.3) | data formatting | bytes 4194304 | tf_op jit(solution)/shard_map/mul | solution.py:21
  98.3 3.0 %copy.33 = f32[128,4096]{1,0:T(8,128)} copy(f32[128,4096]{0,1:T(8,128)} %bitcast.64) | data formatting | bytes 4194304 | tf_op jit(solution)/shard_map/mul | solution.py:21
  101.3 3.6 %convolution_add_fusion.4 = f32[128,4096]{1,0:T(8,128)S(1)} fusion(f32[128,4096]{1,0:T(8,128)} %copy.33, f32[128,128]{1,0:T(8,128)S(1)} %fusion.11, f32[128,4096]{0,1:T(8,128)S(1)} %bitcast.62), kind=kOutput, calls=%fused_computation.5 | convolution fusion | flops 805830656 | bytes 6356992 | tf_op jit(solution)/shard_map/mij,mjk->mik/dot_general | solution.py:21
  104.9 1.8 fusion.13
  106.9 2.0 convolution_add_fusion.3
  108.9 1.8 fusion.14
  110.9 2.0 convolution_add_fusion.2
  113.0 1.8 fusion.15
  115.0 2.3 %convolution_add_fusion.1 = f32[128,4096]{1,0:T(8,128)S(1)} fusion(f32[128,128]{1,0:T(8,128)S(1)} %fusion.8, f32[128,4096]{1,0:T(8,128)S(1)} %convolution_add_fusion.2), kind=kOutput, calls=%fused_computation.2 | convolution fusion | flops 806354944 | bytes 4259840 | tf_op jit(solution)/shard_map/mij,mjk->mik/dot_general | solution.py:21
  117.3 1.8 fusion.16
  119.3 2.0 fusion
  121.3 3.7 %copy.34 = f32[1,128,4096]{1,0,2:T(1,128)} copy(f32[1,128,4096]{2,1,0:T(8,128)S(1)} %fusion) | data formatting | bytes 4194304 | tf_op jit(solution)/shard_map/add | solution.py:21
  125.0 29.2 %all_to_all.65 = f32[1,128,4096]{1,0,2:T(1,128)S(1)} all-to-all(f32[1,128,4096]{1,0,2:T(1,128)} %copy.34), channel_id=1, replica_groups=mesh['fsdp'=8,'tp'=4] {'tp'}, dimensions={2} | all-to-all | bytes 4194304 | tf_op jit(solution)/shard_map/all_to_all | solution.py:24
  154.3 2.0 copy.35
  156.2 51.7 %all_to_all.66 = f32[4,128,1024]{2,0,1:T(4,128)S(1)} all-to-all(f32[4,128,1024]{2,0,1:T(4,128)} %copy.35), channel_id=1, replica_groups=mesh['fsdp'=8,'tp'=4] {'fsdp'}, dimensions={1} | all-to-all | bytes 4194304 | tf_op jit(solution)/shard_map/all_to_all | solution.py:25
  207.9 1.2 copy.36
  209.4 1.3 copy-done.1
  210.7 1.7 bitcast_subtract_fusion
  (11 shorter events, 2.6 us)
Async XLA Ops:
  3.3 55.3 %copy-start = (f32[32,16,1024]{2,1,0:T(8,128)}, f32[32,16,1024]{2,1,0:T(8,128)S(1)}, u32[]{:S(2)}) copy-start(f32[32,16,1024]{2,1,0:T(8,128)S(1)} %multiply_add_fusion) | copy-start | bytes 6291460
  209.1 1.6 copy-start.1
where the time goes:
time: 213 us; the launch traced here: 212 us
  blocking collectives  164 us (77%)
  matrix products  22 us (10%)
  local copies, waits for them, and re-layouts  16.4 us (8%)
  other arithmetic  8.09 us (4%)
    all_to_all x1, blocking collectives, body(): lax.all_to_all(new_momentum, 'fsdp', split_axis=0, concat_axis=1, tiled=T...  55.3 us
    all_to_all x1, blocking collectives, body(): lax.all_to_all(iterate, 'fsdp', split_axis=1, concat_axis=0, tiled=True)  51.7 us
    all_to_all x1, blocking collectives, body(): lax.all_to_all(iterate, 'tp', split_axis=2, concat_axis=0, tiled=True)  29.2 us
    all_to_all x1, blocking collectives, body(): whole = lax.all_to_all(moved, 'tp', split_axis=0, concat_axis=2, tiled=True)  28.3 us
    dot_general x5, matrix products, body(): jnp.einsum('mij,mjk->mik', mixed, iterate, precision=lax.Precision.HIGHEST)  12 us
    dot_general x5, matrix products, body(): jnp.einsum('mik,mjk->mij', iterate, iterate, precision=lax.Precision.HIGH...  8.96 us
    mul x2, local copies, waits for them, and re-layouts, body(): 3.4445 * iterate  5.84 us

commit v1 on v0

--- a/solution.py
+++ b/solution.py
@@ -21,7 +21,10 @@
         iterate = 3.4445 * iterate + jnp.einsum(
             "mij,mjk->mik", mixed, iterate, precision=lax.Precision.HIGHEST
         )
-    iterate = lax.all_to_all(iterate, "tp", split_axis=2, concat_axis=0, tiled=True)
+    iterate = jnp.concatenate(
+        lax.all_to_all(jnp.stack(jnp.split(iterate, lax.axis_size("tp"), axis=2)), "tp", 0, 0),
+        axis=0,
+    )
     back = lax.all_to_all(iterate, "fsdp", split_axis=1, concat_axis=0, tiled=True)
     new_weights = weights_in - learn_rate * back
     return (new_weights, new_momentum)

time: 213 us -> 206 us (0.967)
  local copies, waits for them, and re-layouts: 16.4 us -> 11.1 us
    add x1 -> x0, local copies, waits for them, and re-layouts: 3.7 us -> none  [body(): 3.4445 * iterate]
where the time goes in v1:
time: 206 us
  blocking collectives  163 us (79%)
  matrix products  22 us (11%)
  local copies, waits for them, and re-layouts  11.1 us (5%)
  other arithmetic  8.32 us (4%)
    all_to_all x1, blocking collectives, body(): lax.all_to_all(new_momentum, 'fsdp', split_axis=0, concat_axis=1, tiled=T...  55.3 us
    all_to_all x1, blocking collectives, body(): lax.all_to_all(iterate, 'fsdp', split_axis=1, concat_axis=0, tiled=True)  51.4 us
    all_to_all x1, blocking collectives, body(): whole = lax.all_to_all(moved, 'tp', split_axis=0, concat_axis=2, tiled=True)  28.3 us
    all_to_all x1, blocking collectives, body(): lax.all_to_all(jnp.stack(jnp.split(iterate, lax.axis_size('tp'), axis=2))...  28.1 us
    dot_general x5, matrix products, body(): jnp.einsum('mij,mjk->mik', mixed, iterate, precision=lax.Precision.HIGHEST)  12 us
    dot_general x5, matrix products, body(): jnp.einsum('mik,mjk->mij', iterate, iterate, precision=lax.Precision.HIGH...  8.96 us
    mul x2, local copies, waits for them, and re-layouts, body(): 3.4445 * iterate  5.8 us

profile of v1, /device:TPU:0, one launch (start us, length us, event | category | flops | bytes accessed | tf_op | source)
XLA Modules:
  0.0 206.0 jit_solution(1334329843250225756)
XLA Ops:
  0.6 2.7 %multiply_add_fusion = f32[32,16,1024]{2,1,0:T(8,128)S(1)} fusion(f32[32,16,1024]{2,1,0:T(8,128)} %param.3, f32[32,16,1024]{2,1,0:T(8,128)} %param.4), kind=kLoop, calls=%fused_computation.12 | loop fusion | flops 1048576 | bytes 6291456 | tf_op jit(solution)/shard_map/add | solution.py:12
  3.3 55.3 %all_to_all.50 = f32[32,16,1024]{2,1,0:T(8,128)S(1)} all-to-all(f32[32,16,1024]{2,1,0:T(8,128)S(1)} %multiply_add_fusion), channel_id=1, replica_groups=mesh['fsdp'=8,'tp'=4] {'fsdp'}, dimensions={0} | all-to-all | bytes 4194304 | tf_op jit(solution)/shard_map/all_to_all | solution.py:13
  58.9 28.3 %all_to_all.51 = f32[4,128,1024]{2,1,0:T(8,128)S(1)} all-to-all(f32[4,128,1024]{2,1,0:T(8,128)S(1)} %bitcast.67), channel_id=1, replica_groups=mesh['fsdp'=8,'tp'=4] {'tp'}, dimensions={0} | all-to-all | bytes 4194304 | tf_op jit(solution)/shard_map/all_to_all | solution.py:14
  87.1 1.1 multiply_reduce_fusion
  88.9 1.8 fusion.4
  91.0 2.6 %multiply_bitcast_fusion.1 = (f32[1,128,4,1024]{3,1,2,0:T(8,128)}, f32[1,128,4,1024]{3,1,2,0:T(8,128)}) fusion(f32[4,128,1024]{2,1,0:T(8,128)S(1)} %all_to_all.51, f32[]{:T(128)S(6)} %rsqrt.4), kind=kLoop, calls=%fused_computation.14 | loop fusion | flops 1048576 | bytes 6291460 | tf_op jit(solution)/shard_map/mul | solution.py:15
  93.5 1.9 copy.14
  95.4 2.9 %copy.13 = f32[1,128,4,1024]{1,3,2,0:T(8,128)} copy(f32[1,128,4,1024]{3,1,2,0:T(8,128)} %get-tuple-element.7) | data formatting | bytes 4194304 | tf_op jit(solution)/shard_map/mul | solution.py:21
  98.3 2.9 %copy.15 = f32[128,4096]{1,0:T(8,128)} copy(f32[128,4096]{0,1:T(8,128)} %bitcast.68) | data formatting | bytes 4194304 | tf_op jit(solution)/shard_map/mul | solution.py:21
  101.2 3.6 %convolution_add_fusion.4 = f32[128,4096]{1,0:T(8,128)S(1)} fusion(f32[128,4096]{1,0:T(8,128)} %copy.15, f32[128,128]{1,0:T(8,128)S(1)} %fusion.11, f32[128,4096]{0,1:T(8,128)S(1)} %bitcast.66), kind=kOutput, calls=%fused_computation.5 | convolution fusion | flops 805830656 | bytes 6356992 | tf_op jit(solution)/shard_map/mij,mjk->mik/dot_general | solution.py:21
  104.8 1.8 fusion.13
  106.8 2.0 convolution_add_fusion.3
  108.9 1.8 fusion.14
  110.9 2.0 convolution_add_fusion.2
  112.9 1.8 fusion.15
  114.9 2.3 %convolution_add_fusion.1 = f32[128,4096]{1,0:T(8,128)S(1)} fusion(f32[128,128]{1,0:T(8,128)S(1)} %fusion.8, f32[128,4096]{1,0:T(8,128)S(1)} %convolution_add_fusion.2), kind=kOutput, calls=%fused_computation.2 | convolution fusion | flops 806354944 | bytes 4259840 | tf_op jit(solution)/shard_map/mij,mjk->mik/dot_general | solution.py:21
  117.2 1.8 fusion.16
  119.3 2.0 fusion
  121.8 28.1 %all_to_all.52 = f32[4,1,128,1024]{3,2,1,0:T(8,128)S(1)} all-to-all(f32[4,1,128,1024]{3,2,1,0:T(8,128)S(1)} %pad_maximum_fusion), channel_id=1, replica_groups=mesh['fsdp'=8,'tp'=4] {'tp'}, dimensions={0} | all-to-all | bytes 4194304 | tf_op jit(solution)/shard_map/all_to_all | solution.py:25
  149.9 1.4 copy.16
  151.3 51.4 %all_to_all.53 = f32[4,128,1024]{2,0,1:T(4,128)S(1)} all-to-all(f32[4,128,1024]{2,0,1:T(4,128)S(1)} %copy.16), channel_id=1, replica_groups=mesh['fsdp'=8,'tp'=4] {'fsdp'}, dimensions={1} | all-to-all | bytes 4194304 | tf_op jit(solution)/shard_map/all_to_all | solution.py:28
  202.6 1.2 copy.17
  203.8 0.4 copy-done.1
  204.2 1.7 bitcast_subtract_fusion
  (11 shorter events, 1.8 us)
Async XLA Ops:
  3.3 55.3 %copy-start = (f32[32,16,1024]{2,1,0:T(8,128)}, f32[32,16,1024]{2,1,0:T(8,128)S(1)}, u32[]{:S(2)}) copy-start(f32[32,16,1024]{2,1,0:T(8,128)S(1)} %multiply_add_fusion) | copy-start | bytes 6291460
  202.6 1.6 copy-start.1
